TPU v7x, 32 devices: a whole 2x2x4 slice. The times are simulated.
32 devices in a mesh: beam: 2 (over x), pulse: 16 (over z, y, core).
Axes of the slice: x: 2, y: 2, z: 4, core: 2. Of those that a mesh axis runs over, the one named last changes fastest.
Arguments:
- echoes: float32 [2, 4096, 1536], P(None, 'pulse', 'beam'), parts along dimension 2, may hold values from -6 to 6
- guard_gates: int32 [1], replicated, may hold values from 1 to 4
- train_gates: int32 [1], replicated, may hold values from 4 to 16
Outputs:
- powers: float32 [4096, 1536], P('pulse', 'beam'), parts along dimension 1
- statistic: float32 [4096, 1536], P('pulse', 'beam'), parts along dimension 1
There are 2 independent parts, one for each index of `beam`. A program takes and returns all parts, laid end to end along the dimension named above; an argument that names none is the same for every part. Nothing has to cross between parts.
All inputs are finite; a program needn't handle non-finite values.
Results may differ from a plain program's by a relative error of at most 0.0003.
Values sent between devices are 32-bit elements; how exact they have to be, the bound alone decides.
No kernel may reach another device: no remote copies, remote signals or barrier semaphores. Data moves between devices by JAX's collectives and lax.ppermute only.
A program may use at most 192 MiB of HBM per device.

v0:
```python
import jax
import jax.numpy as jnp
from jax import lax
from jax.sharding import PartitionSpec as P

PULSES = 4096
GUARD_BINS = 2
TRAIN_BINS = 4


TWO_PI = 6.283185307179586


def padded_2(cells, sides, width):
    for axis, dim in sides:
        count = lax.axis_size(axis)
        head = lax.slice_in_dim(cells, 0, width, axis=dim)
        tail = lax.slice_in_dim(cells, cells.shape[dim] - width, cells.shape[dim], axis=dim)
        cells = jnp.concatenate(
            [
                lax.ppermute(tail, axis, [(i, (i + 1) % count) for i in range(count)]),
                cells,
                lax.ppermute(head, axis, [((i + 1) % count, i) for i in range(count)]),
            ],
            axis=dim,
        )
    return cells


def small_tables(count):
    index_row = jnp.arange(count, dtype=jnp.int32)
    phases = (index_row[:, None] * index_row[None, :] % count).astype(jnp.float32) * (
        TWO_PI / count
    )
    return (jnp.cos(phases), jnp.sin(phases))


def product(left, right):
    return jnp.dot(left, right, precision=lax.Precision.HIGHEST, preferred_element_type=jnp.float32)


def factored_powers(samples):
    width = samples.shape[2]
    bit_count = PULSES.bit_length() - 1
    first_radix = 2 ** (bit_count // 2)
    second_radix = PULSES // first_radix
    cos_first, sin_first = small_tables(first_radix)
    real_in = samples[0].reshape(first_radix, second_radix * width)
    imag_in = samples[1].reshape(first_radix, second_radix * width)
    real_one = (product(cos_first, real_in) + product(sin_first, imag_in)).reshape(
        first_radix, second_radix, width
    )
    imag_one = (product(cos_first, imag_in) - product(sin_first, real_in)).reshape(
        first_radix, second_radix, width
    )
    first_ids = jnp.arange(first_radix, dtype=jnp.int32)
    second_ids = jnp.arange(second_radix, dtype=jnp.int32)
    twist = (first_ids[:, None] * second_ids[None, :] % PULSES).astype(jnp.float32) * (
        TWO_PI / PULSES
    )
    twist_cos = jnp.cos(twist)[:, :, None]
    twist_sin = jnp.sin(twist)[:, :, None]
    real_two = twist_cos * real_one + twist_sin * imag_one
    imag_two = twist_cos * imag_one - twist_sin * real_one
    real_two = jnp.transpose(real_two, (1, 0, 2)).reshape(second_radix, first_radix * width)
    imag_two = jnp.transpose(imag_two, (1, 0, 2)).reshape(second_radix, first_radix * width)
    cos_second, sin_second = small_tables(second_radix)
    scale_factor = 1.0 / jnp.sqrt(jnp.float32(PULSES))
    real_out = (product(cos_second, real_two) + product(sin_second, imag_two)) * scale_factor
    imag_out = (product(cos_second, imag_two) - product(sin_second, real_two)) * scale_factor
    result = real_out * real_out + imag_out * imag_out
    return result.reshape(PULSES, width)


def shards(echoes, guard_gates, train_gates):
    devices_count = lax.axis_size("pulse")
    bins_local = PULSES // devices_count
    gates_count = echoes.shape[2]
    columns = factored_powers(
        lax.all_to_all(echoes, "pulse", split_axis=2, concat_axis=1, tiled=True)
    )
    powers = lax.all_to_all(columns, "pulse", split_axis=0, concat_axis=1, tiled=True)
    reach = GUARD_BINS + TRAIN_BINS
    padded = padded_2(powers, (("pulse", 0),), reach)
    doppler_sum = jnp.zeros_like(powers)
    for shift_bins in range(GUARD_BINS + 1, reach + 1):
        above = padded[reach + shift_bins : reach + shift_bins + bins_local]
        below = padded[reach - shift_bins : reach - shift_bins + bins_local]
        doppler_sum = doppler_sum + above + below
    guard_width = guard_gates[0]
    train_width = train_gates[0]
    gate_ids = jnp.arange(gates_count, dtype=jnp.int32)
    offsets = jnp.abs(gate_ids[:, None] - gate_ids[None, :])
    band = ((offsets > guard_width) & (offsets <= guard_width + train_width)).astype(jnp.float32)
    range_sum = jnp.dot(
        powers, band, precision=lax.Precision.HIGHEST, preferred_element_type=jnp.float32
    )
    range_count = jnp.sum(band, axis=0)
    noise_level = (range_sum + doppler_sum) / (range_count[None, :] + 2.0 * TRAIN_BINS)
    statistic = powers / (noise_level + 1.0)
    return (powers, statistic)


def solution(mesh):
    return jax.shard_map(
        shards,
        mesh=mesh,
        in_specs=(P(None, "pulse", "beam"), P(), P()),
        out_specs=(P("pulse", "beam"), P("pulse", "beam")),
        check_vma=False,
    )
```

profile of v0, /device:TPU:0, one launch (start us, length us, event | category | flops | bytes accessed | tf_op | source)
XLA Modules:
  0.0 128.5 jit_solution(2452970888408496449)
XLA Ops:
  0.6 3.7 %copy.33 = f32[2,256,768]{1,0,2:T(2,128)} copy(f32[2,256,768]{2,1,0:T(8,128)} %param.3) | data formatting | bytes 3145728 | tf_op args[0]
  4.3 7.4 %all-to-all-start = ((f32[2,256,768]{1,0,2:T(2,128)}), f32[2,256,768]{1,0,2:T(2,128)S(1)}, u32[]{:S(2)}, u32[]{:S(2)}) async-start(f32[2,256,768]{1,0,2:T(2,128)} %copy.33), calls=%async_computation | async-start | bytes 3145728 | tf_op jit(solution)/shard_map/all_to_all | solution.py:80
  11.9 31.7 %all-to-all-done = f32[2,256,768]{1,0,2:T(2,128)S(1)} async-done(((f32[2,256,768]{1,0,2:T(2,128)}), f32[2,256,768]{1,0,2:T(2,128)S(1)}, u32[]{:S(2)}, u32[]{:S(2)}) %all-to-all-start) | async-done | bytes 1572896 | tf_op jit(solution)/shard_map/all_to_all | solution.py:80
  43.7 1.0 fusion.84
  44.7 0.6 copy.36
  45.3 1.8 %reshape_squeeze.7 = f32[64,3072]{1,0:T(8,128)S(1)} reshape(f32[1,16,256,48]{3,2,1,0:T(8,128)S(1)} %copy.36) | data formatting | bytes 1572864 | tf_op jit(solution)/shard_map/reshape;squeeze | solution.py:49
  47.1 1.8 %fusion.44 = f32[64,3072]{1,0:T(8,128)} fusion(f32[64,3072]{1,0:T(8,128)S(1)} %reshape_squeeze.7), kind=kOutput, calls=%fused_computation.66 | convolution fusion | flops 151052288 | bytes 1572864 | tf_op jit(solution)/shard_map/dot_general | solution.py:39
  48.9 1.7 %copy.35 = f32[1,16,256,48]{3,2,1,0:T(8,128)S(1)} copy(f32[1,16,256,48]{2,3,1,0:T(8,128)} %get-tuple-element.10) | data formatting | bytes 1572864 | tf_op jit(solution)/shard_map/slice | solution.py:48
  50.6 2.7 %reshape_squeeze.6 = f32[64,3072]{1,0:T(8,128)} reshape(f32[1,16,256,48]{3,2,1,0:T(8,128)S(1)} %copy.35) | data formatting | bytes 1572864 | tf_op jit(solution)/shard_map/reshape;squeeze | solution.py:48
  53.3 3.0 %fusion.46 = f32[64,3072]{1,0:T(8,128)} fusion(f32[64,3072]{1,0:T(8,128)} %reshape_squeeze.6), kind=kOutput, calls=%fused_computation.67 | convolution fusion | flops 151052288 | bytes 1572864 | tf_op jit(solution)/shard_map/dot_general | solution.py:39
  56.4 1.8 %convolution_subtract_fusion.1 = f32[64,3072]{1,0:T(8,128)} fusion(f32[64,3072]{1,0:T(8,128)S(1)} %copy-done.2, f32[64,3072]{1,0:T(8,128)S(1)} %copy-done), kind=kOutput, calls=%fused_computation.2 | convolution fusion | flops 151248896 | bytes 2359296 | tf_op jit(solution)/shard_map/dot_general | solution.py:39
  58.2 2.0 %reshape.68 = f32[64,64,48]{2,1,0:T(8,128)S(1)} reshape(f32[64,3072]{1,0:T(8,128)} %convolution_subtract_fusion.1) | data formatting | bytes 1572864 | tf_op jit(solution)/shard_map/reshape | solution.py:53
  60.2 2.9 %convolution_add_fusion.1 = f32[64,3072]{1,0:T(8,128)} fusion(f32[64,3072]{1,0:T(8,128)} %fusion.46, f32[64,3072]{1,0:T(8,128)S(1)} %reshape_squeeze.7), kind=kOutput, calls=%fused_computation.3 | convolution fusion | flops 151248896 | bytes 2359296 | tf_op jit(solution)/shard_map/dot_general | solution.py:39
  63.1 3.1 %reshape.67 = f32[64,64,48]{2,1,0:T(8,128)} reshape(f32[64,3072]{1,0:T(8,128)} %convolution_add_fusion.1) | data formatting | bytes 1572864 | tf_op jit(solution)/shard_map/reshape | solution.py:50
  66.2 4.2 %subtract_bitcast_fusion = (f32[64,64,48]{2,0,1:T(8,128)}, f32[64,64,48]{2,0,1:T(8,128)S(1)}) fusion(f32[64,64,48]{2,1,0:T(8,128)} %reshape.67, f32[64,64,48]{2,1,0:T(8,128)S(1)} %reshape.68, f32[64,64]{1,0:T(8,128)S(1)} %get-tuple-element.14, f32[64,64]{1,0:T(8,128)S(1)} %get-tuple-element.15), kind=kLoop, calls=%fused_computation.14 | loop fusion | flops 1179648 | bytes 3178496 | tf_op jit(solution)/shard_map/transpose | solution.py:66
  70.5 1.2 copy.37
  71.7 1.8 %reshape.69 = f32[64,3072]{1,0:T(8,128)S(1)} reshape(f32[64,64,48]{2,1,0:T(8,128)S(1)} %copy.37) | data formatting | bytes 1572864 | tf_op jit(solution)/shard_map/reshape | solution.py:65
  73.4 1.8 %fusion.42 = f32[64,3072]{1,0:T(8,128)} fusion(f32[64,3072]{1,0:T(8,128)S(1)} %reshape.69), kind=kOutput, calls=%fused_computation.65 | convolution fusion | flops 151052288 | bytes 1572864 | tf_op jit(solution)/shard_map/dot_general | solution.py:39
  75.3 2.8 %copy.38 = f32[64,64,48]{2,1,0:T(8,128)S(1)} copy(f32[64,64,48]{2,0,1:T(8,128)} %get-tuple-element.8) | data formatting | bytes 1572864 | tf_op jit(solution)/shard_map/transpose | solution.py:66
  78.1 2.7 %reshape.70 = f32[64,3072]{1,0:T(8,128)} reshape(f32[64,64,48]{2,1,0:T(8,128)S(1)} %copy.38) | data formatting | bytes 1572864 | tf_op jit(solution)/shard_map/reshape | solution.py:66
  80.7 2.2 %fusion.40 = f32[64,3072]{1,0:T(8,128)S(1)} fusion(f32[64,3072]{1,0:T(8,128)} %reshape.70), kind=kOutput, calls=%fused_computation.64 | convolution fusion | flops 151052288 | bytes 1572864 | tf_op jit(solution)/shard_map/dot_general | solution.py:39
  82.9 1.0 fusion.1
  83.9 1.0 fusion.4
  84.9 0.9 all_to_all.28
  85.8 1.5 %copy.39 = f32[16,256,48]{1,2,0:T(8,128)} copy(f32[16,256,48]{2,1,0:T(8,128)S(1)} %all_to_all.28) | data formatting | bytes 1572864 | tf_op jit(solution)/shard_map/all_to_all | solution.py:82
  87.2 9.1 %all-to-all-start.1 = ((f32[16,256,48]{1,2,0:T(8,128)}), f32[16,256,48]{1,2,0:T(8,128)S(1)}, u32[]{:S(2)}, u32[]{:S(2)}) async-start(f32[16,256,48]{1,2,0:T(8,128)} %copy.39), calls=%async_computation.1 | async-start | bytes 1572864 | tf_op jit(solution)/shard_map/all_to_all | solution.py:82
  97.7 0.6 convert_reduce_fusion
  98.3 16.8 %all-to-all-done.1 = f32[16,256,48]{1,2,0:T(8,128)S(1)} async-done(((f32[16,256,48]{1,2,0:T(8,128)}), f32[16,256,48]{1,2,0:T(8,128)S(1)}, u32[]{:S(2)}, u32[]{:S(2)}) %all-to-all-start.1) | async-done | bytes 786464 | tf_op jit(solution)/shard_map/all_to_all | solution.py:82
  115.4 4.0 %collective-permute-start = (f32[6,768]{1,0:T(8,128)S(1)}, f32[6,768]{1,0:T(8,128)S(1)}, u32[]{:S(2)}, u32[]{:S(2)}) collective-permute-start(f32[6,768]{1,0:T(8,128)S(1)} %copy.46), channel_id=1, source_target_pairs={{1,0},{2,1},{3,2},{4,3},{5,4},{6,5},{7,6},{8,7},{9,8},{10,9},{11,1... | collective-permute-start | bytes 55304 | tf_op jit(solution)/shard_map/ppermute | solution.py:23
  119.9 1.0 collective-permute-done
  120.9 4.6 %collective-permute-done.1 = f32[6,768]{1,0:T(8,128)S(1)} collective-permute-done((f32[6,768]{1,0:T(8,128)S(1)}, f32[6,768]{1,0:T(8,128)S(1)}, u32[]{:S(2)}, u32[]{:S(2)}) %collective-permute-start.1) | collective-permute-done | bytes 18464 | tf_op jit(solution)/shard_map/ppermute | solution.py:21
  125.5 3.0 %add_divide_fusion = f32[256,768]{1,0:T(8,128)} fusion(f32[256,768]{1,0:T(8,128)S(1)} %copy.45, f32[6,768]{1,0:T(8,128)S(1)} %collective-permute-done.1, f32[6,768]{1,0:T(8,128)S(1)} %collective-permute-done, f32[768]{0:T(1024)S(1)} %broadcast_add_fusion, f32[256,768]{0,1:T(8,128)S(1)} %bitcast.33, s32[]{:T(128)S(6)} %add.101, s32[]{:T(128)} %bitcast.27), kind=kOutput, calls=%fused_computation.42 | convolution fusion | flops 1818624000 | bytes 2399240 | tf_op jit(solution)/shard_map/dot_general | solution.py:95
  (18 shorter events, 1.0 us)
Async XLA Ops:
  4.3 39.3 %all-to-all-start = ((f32[2,256,768]{1,0,2:T(2,128)}), f32[2,256,768]{1,0,2:T(2,128)S(1)}, u32[]{:S(2)}, u32[]{:S(2)}) async-start(f32[2,256,768]{1,0,2:T(2,128)} %copy.33), calls=%async_computation | async-start | bytes 3145728 | tf_op jit(solution)/shard_map/all_to_all | solution.py:80
  53.3 3.0 %copy-start = (f32[64,3072]{1,0:T(8,128)S(1)}, f32[64,3072]{1,0:T(8,128)}, u32[]{:S(2)}) copy-start(f32[64,3072]{1,0:T(8,128)} %reshape_squeeze.6) | copy-start | bytes 2359300
  53.3 3.0 %copy-start.2 = (f32[64,3072]{1,0:T(8,128)S(1)}, f32[64,3072]{1,0:T(8,128)}, u32[]{:S(2)}) copy-start(f32[64,3072]{1,0:T(8,128)} %fusion.44) | copy-start | bytes 2359300
  80.7 2.2 %copy-start.1 = (f32[64,3072]{1,0:T(8,128)S(1)}, f32[64,3072]{1,0:T(8,128)}, u32[]{:S(2)}) copy-start(f32[64,3072]{1,0:T(8,128)} %reshape.70) | copy-start | bytes 2359300
  80.7 2.2 %copy-start.3 = (f32[64,3072]{1,0:T(8,128)S(1)}, f32[64,3072]{1,0:T(8,128)}, u32[]{:S(2)}) copy-start(f32[64,3072]{1,0:T(8,128)} %fusion.42) | copy-start | bytes 2359300
  87.2 27.8 %all-to-all-start.1 = ((f32[16,256,48]{1,2,0:T(8,128)}), f32[16,256,48]{1,2,0:T(8,128)S(1)}, u32[]{:S(2)}, u32[]{:S(2)}) async-start(f32[16,256,48]{1,2,0:T(8,128)} %copy.39), calls=%async_computation.1 | async-start | bytes 1572864 | tf_op jit(solution)/shard_map/all_to_all | solution.py:82
  115.4 5.5 %collective-permute-start = (f32[6,768]{1,0:T(8,128)S(1)}, f32[6,768]{1,0:T(8,128)S(1)}, u32[]{:S(2)}, u32[]{:S(2)}) collective-permute-start(f32[6,768]{1,0:T(8,128)S(1)} %copy.46), channel_id=1, source_target_pairs={{1,0},{2,1},{3,2},{4,3},{5,4},{6,5},{7,6},{8,7},{9,8},{10,9},{11,1... | collective-permute-start | bytes 55304 | tf_op jit(solution)/shard_map/ppermute | solution.py:23
  119.5 6.0 %collective-permute-start.1 = (f32[6,768]{1,0:T(8,128)S(1)}, f32[6,768]{1,0:T(8,128)S(1)}, u32[]{:S(2)}, u32[]{:S(2)}) collective-permute-start(f32[6,768]{1,0:T(8,128)S(1)} %copy.47), channel_id=1, source_target_pairs={{0,1},{1,2},{2,3},{3,4},{4,5},{5,6},{6,7},{7,8},{8,9},{9,10},{10,1... | collective-permute-start | bytes 55304 | tf_op jit(solution)/shard_map/ppermute | solution.py:21
  119.8 8.7 %copy-start.4 = (f32[256,768]{1,0:T(8,128)}, f32[256,768]{1,0:T(8,128)S(1)}, u32[]{:S(2)}) copy-start(f32[256,768]{1,0:T(8,128)S(1)} %copy.45) | copy-start | bytes 2359300
where the time goes:
time: 129 us
  waiting for transfers between devices  54.1 us (42%)
  local copies, waits for them, and re-layouts  28.2 us (22%)
  starting transfers between devices  20.6 us (16%)
  matrix products  18.6 us (14%)
  other arithmetic  5 us (4%)
  between operations  2.08 us (2%)
    all_to_all x1, waiting for transfers between devices, shards(): lax.all_to_all(echoes, 'pulse', split_axis=2, concat_axis=1, tiled=True)  31.7 us
    all_to_all x1, waiting for transfers between devices, shards(): lax.all_to_all(columns, 'pulse', split_axis=0, concat_axis=1, tiled=True)  16.8 us
    dot_general x8, matrix products, product(): jnp.dot(left, right, precision=lax.Precision.HIGHEST, preferred_element_t...  15.5 us
    all_to_all x1, starting transfers between devices, shards(): lax.all_to_all(columns, 'pulse', split_axis=0, concat_axis=1, tiled=True)  9.12 us
    all_to_all x1, starting transfers between devices, shards(): lax.all_to_all(echoes, 'pulse', split_axis=2, concat_axis=1, tiled=True)  7.41 us
    ppermute x1, waiting for transfers between devices, padded_2(): lax.ppermute(tail, axis, [(i, (i + 1) % count) for i in range(count)])  4.6 us
    transpose x1, other arithmetic, factored_powers(): jnp.transpose(imag_two, (1, 0, 2))  4.25 us
    ppermute x1, starting transfers between devices, padded_2(): lax.ppermute(head, axis, [((i + 1) % count, i) for i in range(count)])  4.02 us
  transfers between devices with their start and end apart: 4, of which 4 were waited for; matrix products, arithmetic and copies ran while one was open for 1% of the time, Pallas kernels for 0%

commit v1 on v0

--- a/solution.py
+++ b/solution.py
@@ -1,11 +1,18 @@
 import jax
 import jax.numpy as jnp
+import numpy as np
 from jax import lax
+from jax.experimental import pallas as pl
+from jax.experimental.pallas import tpu as pltpu
 from jax.sharding import PartitionSpec as P
 
 PULSES = 4096
 GUARD_BINS = 2
 TRAIN_BINS = 4
+LANES = 128
+SUBLANES = 8
+EDGE = 8
+CHUNKS = (3, 3)
 
 
 TWO_PI = 6.283185307179586
@@ -72,7 +79,7 @@
     return result.reshape(PULSES, width)
 
 
-def shards(echoes, guard_gates, train_gates):
+def plain_shards(echoes, guard_gates, train_gates):
     devices_count = lax.axis_size("pulse")
     bins_local = PULSES // devices_count
     gates_count = echoes.shape[2]
@@ -101,6 +108,246 @@
     return (powers, statistic)
 
 
+def host_tables(devices, local):
+    q = np.arange(local)
+    angle = 2.0 * np.pi * np.outer(np.arange(devices), q) / PULSES
+    scale = 1.0 / np.sqrt(PULSES)
+    twist = np.stack([np.cos(angle) * scale, np.sin(angle) * scale]).astype(np.float32)
+    phase = 2.0 * np.pi * (np.outer(q, q) % local) / local
+    cosine, sine = np.cos(phase), np.sin(phase)
+    both = np.concatenate(
+        [np.concatenate([cosine, -sine], axis=1), np.concatenate([sine, cosine], axis=1)], axis=0
+    ).astype(np.float32)
+    high = both.astype(jnp.bfloat16)
+    low = (both - high.astype(np.float32)).astype(jnp.bfloat16)
+    return twist, high, low
+
+
+def spread_kernel(x_ref, o_ref):
+    parts, local, lanes = x_ref.shape
+    devices = o_ref.shape[0]
+    for part in range(parts):
+        for start in range(0, local, LANES):
+            turned = x_ref[part, start : start + LANES, :].T
+            at = part * local + start
+            o_ref[:, :, at : at + LANES] = turned.reshape(devices, SUBLANES, LANES)
+
+
+def spread(echoes, devices, first, count):
+    parts, local, _ = echoes.shape
+    return pl.pallas_call(
+        spread_kernel,
+        grid=(count,),
+        in_specs=[pl.BlockSpec((parts, local, LANES), lambda t: (0, 0, first + t))],
+        out_specs=pl.BlockSpec((devices, SUBLANES, parts * local), lambda t: (0, t, 0)),
+        out_shape=jax.ShapeDtypeStruct((devices, SUBLANES * count, parts * local), jnp.float32),
+    )(echoes)
+
+
+def rotate(real, imag, turn, count):
+    if turn == 0:
+        return real, imag
+    if 4 * turn == count:
+        return imag, -real
+    cos, sin = float(np.cos(2 * np.pi * turn / count)), float(np.sin(2 * np.pi * turn / count))
+    if 8 * turn == count:
+        return (real + imag) * cos, (imag - real) * cos
+    if 8 * turn == 3 * count:
+        return (imag - real) * sin, (real + imag) * (-sin)
+    return real * cos + imag * sin, imag * cos - real * sin
+
+
+def radix(values):
+    count = len(values)
+    if count == 1:
+        return values
+    even, odd = radix(values[::2]), radix(values[1::2])
+    top, bottom = [], []
+    for i, ((er, ei), (orr, oi)) in enumerate(zip(even, odd)):
+        orr, oi = rotate(orr, oi, i, count)
+        top.append((er + orr, ei + oi))
+        bottom.append((er - orr, ei - oi))
+    return top + bottom
+
+
+def exchange(values, width, lane):
+    values = list(values)
+    step = 1
+    while step < len(values):
+        shift = step * width
+        low_half = (lane // shift) % 2 == 0
+        for i in range(len(values)):
+            if not i & step:
+                a, b = values[i], values[i + step]
+                values[i] = jnp.where(low_half, a, pltpu.roll(b, shift, 1))
+                values[i + step] = jnp.where(low_half, pltpu.roll(a, LANES - shift, 1), b)
+        step *= 2
+    return values
+
+
+def split(value):
+    high = value.astype(jnp.bfloat16)
+    return high, (value - high.astype(jnp.float32)).astype(jnp.bfloat16)
+
+
+def dot(left, right):
+    return jnp.dot(left, right, preferred_element_type=jnp.float32)
+
+
+def transform_kernel(x_ref, twist_ref, high_ref, low_ref, o_ref, z_ref, p_ref):
+    devices, rows, width = x_ref.shape
+    local = width // 2
+    for row in range(0, rows, SUBLANES):
+        for start in range(0, local, LANES):
+            re = slice(start, start + LANES)
+            im = slice(local + start, local + start + LANES)
+            tile = slice(row, row + SUBLANES)
+            values = radix([(x_ref[d, tile, re], x_ref[d, tile, im]) for d in range(devices)])
+            for k0, (real, imag) in enumerate(values):
+                cos = twist_ref[0, k0 : k0 + 1, re]
+                sin = twist_ref[1, k0 : k0 + 1, re]
+                to = slice(k0 * rows + row, k0 * rows + row + SUBLANES)
+                z_ref[to, re] = real * cos + imag * sin
+                z_ref[to, im] = imag * cos - real * sin
+    block = devices * rows // 2
+    for start in range(0, devices * rows, block):
+        high, low = split(z_ref[start : start + block, :])
+        spectrum = dot(high, high_ref[...]) + dot(high, low_ref[...]) + dot(low, high_ref[...])
+        real, imag = spectrum[:, :local], spectrum[:, local:]
+        p_ref[start : start + block, :] = real * real + imag * imag
+    group = local // devices
+    inside = LANES // group
+    halves = local // LANES
+    lane = lax.broadcasted_iota(jnp.int32, (rows, LANES), 1)
+    for upper in range(halves):
+        for half in range(halves):
+            mine = [
+                p_ref[
+                    (upper * inside + i) * rows : (upper * inside + i + 1) * rows,
+                    half * LANES : (half + 1) * LANES,
+                ]
+                for i in range(inside)
+            ]
+            for i, value in enumerate(exchange(mine, group, lane)):
+                o_ref[half * inside + i, upper * rows : (upper + 1) * rows, :] = value
+    wide = lax.broadcasted_iota(jnp.int32, (rows, local), 1) % group
+    edges = jnp.zeros((rows, local), jnp.float32)
+    reach = GUARD_BINS + TRAIN_BINS
+    for j in range(EDGE - reach, EDGE + reach):
+        k0 = devices - EDGE + j if j < EDGE else j - EDGE
+        shift = j + 1 if j < EDGE else local - group + j
+        moved = pltpu.roll(p_ref[k0 * rows : (k0 + 1) * rows, :], shift, 1)
+        edges = jnp.where(wide == j, moved, edges)
+    small = lane[:SUBLANES]
+    for half in range(halves):
+        mine = [edges[row : row + SUBLANES, half * LANES : (half + 1) * LANES] for row in range(0, rows, SUBLANES)]
+        mine += [jnp.zeros((SUBLANES, LANES), jnp.float32)] * (inside - len(mine))
+        for i, value in enumerate(exchange(mine, group, small)):
+            o_ref[half * inside + i, halves * rows : halves * rows + SUBLANES, :] = value
+
+
+def transform(columns, tables):
+    devices, rows, width = columns.shape
+    local = width // 2
+    out_rows = rows * (local // LANES) + SUBLANES
+    return pl.pallas_call(
+        transform_kernel,
+        out_shape=jax.ShapeDtypeStruct((devices, out_rows, LANES), jnp.float32),
+        scratch_shapes=[
+            pltpu.VMEM((devices * rows, width), jnp.float32),
+            pltpu.VMEM((devices * rows, local), jnp.float32),
+        ],
+    )(columns, *tables)
+
+
+def finish_kernel(guard_ref, train_ref, *refs, counts, local, devices):
+    blocks, (powers_ref, statistic_ref, turn_ref, pad_ref) = refs[: len(counts)], refs[len(counts) :]
+    gates = powers_ref.shape[1]
+    group = local // devices
+    halves = local // LANES
+    inside = LANES // group
+    t = 0
+    for count, block in zip(counts, blocks):
+        rows = count * SUBLANES
+        edge = block[:, halves * rows : halves * rows + SUBLANES, :].reshape(LANES, LANES).T
+        for own in range(count):
+            cols = slice(t * LANES, (t + 1) * LANES)
+            for half in range(halves):
+                at = half * rows + own * SUBLANES
+                turn_ref[half, :, :] = block[:, at : at + SUBLANES, :].reshape(LANES, LANES).T
+            for f1 in range(group):
+                for half in range(halves):
+                    tile = turn_ref[half, pl.ds(f1, inside, stride=group), :]
+                    at = f1 * devices + half * inside
+                    powers_ref[at : at + inside, cols] = tile
+                    pad_ref[EDGE + at : EDGE + at + inside, cols] = tile
+            pad_ref[0:EDGE, cols] = edge[own * group : own * group + EDGE, :]
+            pad_ref[EDGE + local : 2 * EDGE + local, cols] = edge[own * group + EDGE : (own + 1) * group, :]
+            t += 1
+    guard, train = guard_ref[0], train_ref[0]
+    source = lax.broadcasted_iota(jnp.int32, (3 * LANES, LANES), 0)
+    target = lax.broadcasted_iota(jnp.int32, (3 * LANES, LANES), 1) + LANES
+    offset = jnp.abs(source - target)
+    band = ((offset > guard) & (offset <= guard + train)).astype(jnp.float32).astype(jnp.bfloat16)
+    total = gates // LANES
+    for t in range(total):
+        cols = slice(t * LANES, (t + 1) * LANES)
+        first, last = max(t - 1, 0), min(t + 2, total)
+        near = powers_ref[:, first * LANES : last * LANES]
+        part = band[(first - t + 1) * LANES : (last - t + 1) * LANES, :]
+        high, low = split(near)
+        sums = dot(high, part) + dot(low, part)
+        pairs = pad_ref[0 : local + 2 * EDGE - 1, cols] + pad_ref[1 : local + 2 * EDGE, cols]
+        fours = pairs[: local + 2 * EDGE - 3] + pairs[2:]
+        near_side = EDGE + GUARD_BINS + 1
+        far_side = EDGE - GUARD_BINS - TRAIN_BINS
+        sums = sums + fours[near_side : near_side + local] + fours[far_side : far_side + local]
+        gate = lax.broadcasted_iota(jnp.int32, (1, LANES), 1) + t * LANES
+        cells = jnp.clip(gate - guard, 0, train) + jnp.clip(gates - 1 - gate - guard, 0, train)
+        noise = sums / (cells.astype(jnp.float32) + 2.0 * TRAIN_BINS)
+        statistic_ref[:, cols] = powers_ref[:, cols] / (noise + 1.0)
+
+
+def finish(blocks, guard_gates, train_gates, counts, local, gates):
+    devices = blocks[0].shape[0]
+    out = jax.ShapeDtypeStruct((local, gates), jnp.float32)
+    vmem = pl.BlockSpec(memory_space=pltpu.VMEM)
+    smem = pl.BlockSpec(memory_space=pltpu.SMEM)
+
+    def body(*refs):
+        finish_kernel(*refs, counts=counts, local=local, devices=devices)
+
+    return pl.pallas_call(
+        body,
+        in_specs=[smem, smem] + [vmem] * len(blocks),
+        out_specs=[vmem, vmem],
+        out_shape=[out, out],
+        scratch_shapes=[
+            pltpu.VMEM((local // LANES, LANES, LANES), jnp.float32),
+            pltpu.VMEM((local + 2 * EDGE, gates), jnp.float32),
+        ],
+    )(guard_gates, train_gates, *blocks)
+
+
+def shards(echoes, guard_gates, train_gates):
+    devices = lax.axis_size("pulse")
+    local, gates = echoes.shape[1:]
+    fits = devices * SUBLANES == LANES and local == devices * 2 * EDGE
+    fits = fits and gates == sum(CHUNKS) * LANES
+    if not fits:
+        return plain_shards(echoes, guard_gates, train_gates)
+    tables = host_tables(devices, local)
+    starts = [sum(CHUNKS[:i]) for i in range(len(CHUNKS))]
+    columns = [
+        lax.all_to_all(spread(echoes, devices, first, count), "pulse", 0, 0, tiled=True)
+        for first, count in zip(starts, CHUNKS)
+    ]
+    blocks = [
+        lax.all_to_all(transform(column, tables), "pulse", 0, 0, tiled=True) for column in columns
+    ]
+    return tuple(finish(blocks, guard_gates, train_gates, CHUNKS, local, gates))
+
+
 def solution(mesh):
     return jax.shard_map(
         shards,

time: 129 us -> 94.2 us (0.73)
  local copies, waits for them, and re-layouts: 28.2 us -> 0.78 us
  matrix products: 18.6 us -> 0 us
  Pallas kernels: 0 us -> 16.3 us
  other arithmetic: 5 us -> 0 us
  waiting for transfers between devices: 54.1 us -> 52.5 us
  starting transfers between devices: 20.6 us -> 22 us
    dot_general x9 -> x0, matrix products: 18.6 us -> none  [the longest x8 15.5 us: product(): jnp.dot(left, right, precision=lax.Precision.HIGHEST, preferred_element_t...]
    pallas_call x0 -> x5, Pallas kernels: none -> 16.3 us  [the longest x2 6.96 us: transform(): pl.pallas_call(transform_kernel, out_shape=jax.ShapeDtypeStruct((devices,...]
    reshape x4 -> x0, local copies, waits for them, and re-layouts: 9.51 us -> none  [the longest x1 3.08 us: factored_powers(): (product(cos_first, real_in) + product(sin_first, imag_in)).reshape(first...]
    ppermute x2 -> x0, waiting for transfers between devices: 5.64 us -> none  [the longest x1 4.6 us: padded_2(): lax.ppermute(tail, axis, [(i, (i + 1) % count) for i in range(count)])]
    all_to_all x2 -> x4, starting transfers between devices: 16.5 us -> 22 us  [the longest x2 12.8 us: shards(): lax.all_to_all(spread(echoes, devices, first, count), 'pulse', 0, 0, tile...]
    another operation x2 -> x0, local copies, waits for them, and re-layouts: 4.43 us -> none  [the longest x1 2.66 us: factored_powers(): real_in = samples[0].reshape(first_radix, second_radix * width)]
    transpose x1 -> x0, other arithmetic: 4.25 us -> none  [factored_powers(): jnp.transpose(imag_two, (1, 0, 2))]
    ppermute x2 -> x0, starting transfers between devices: 4.05 us -> none  [the longest x1 4.02 us: padded_2(): lax.ppermute(head, axis, [((i + 1) % count, i) for i in range(count)])]
  transfers between devices with their start and end apart: 4 -> 4, of which waited for: 4 -> 4; matrix products, arithmetic and copies ran while one was open for 1% -> 0% of each run, Pallas kernels for 0% -> 11%
where the time goes in v1:
time: 94.2 us; the launch traced here: 93.5 us
  waiting for transfers between devices  52.5 us (56%)
  starting transfers between devices  22 us (23%)
  Pallas kernels  16.3 us (17%)
  between operations  1.98 us (2%)
    all_to_all x2, waiting for transfers between devices, shards(): lax.all_to_all(spread(echoes, devices, first, count), 'pulse', 0, 0, tile...  30.8 us
    all_to_all x2, waiting for transfers between devices, shards(): lax.all_to_all(transform(column, tables), 'pulse', 0, 0, tiled=True)  21.7 us
    all_to_all x2, starting transfers between devices, shards(): lax.all_to_all(spread(echoes, devices, first, count), 'pulse', 0, 0, tile...  12.8 us
    all_to_all x2, starting transfers between devices, shards(): lax.all_to_all(transform(column, tables), 'pulse', 0, 0, tiled=True)  9.17 us
    pallas_call x2, Pallas kernels, transform(): pl.pallas_call(transform_kernel, out_shape=jax.ShapeDtypeStruct((devices,...  6.96 us
    pallas_call x2, Pallas kernels, spread(): pl.pallas_call(spread_kernel, grid=(count,), in_specs=[pl.BlockSpec((part...  6.07 us
    pallas_call x1, Pallas kernels, finish(): pl.pallas_call(body, in_specs=[smem, smem] + [vmem] * len(blocks), out_sp...  3.29 us
  transfers between devices with their start and end apart: 4, of which 4 were waited for; matrix products, arithmetic and copies ran while one was open for 0% of the time, Pallas kernels for 11%

profile of v1, /device:TPU:0, one launch (start us, length us, event | category | flops | bytes accessed | tf_op | source)
XLA Modules:
  0.0 93.5 jit_solution(13241490167921004360)
XLA Ops:
  0.6 3.0 %shard_map.79 = f32[16,24,512]{2,1,0:T(8,128)} custom-call(f32[2,256,768]{2,1,0:T(8,128)} %x_ref.3), custom_call_target="tpu_custom_call" | custom-call | tf_op jit(solution)/shard_map/pallas_call | solution.py:138
  3.7 7.4 %all-to-all-start.2 = ((f32[16,24,512]{2,1,0:T(8,128)}), f32[16,24,512]{2,1,0:T(8,128)S(1)}, u32[]{:S(2)}, u32[]{:S(2)}) async-start(f32[16,24,512]{2,1,0:T(8,128)} %shard_map.79), calls=%async_computation.2 | async-start | bytes 1572864 | tf_op jit(solution)/shard_map/all_to_all | solution.py:342
  11.1 3.0 %shard_map.77 = f32[16,24,512]{2,1,0:T(8,128)} custom-call(f32[2,256,768]{2,1,0:T(8,128)} %x_ref.3), custom_call_target="tpu_custom_call" | custom-call | tf_op jit(solution)/shard_map/pallas_call | solution.py:138
  14.1 15.6 %all-to-all-done.2.x_ref = f32[16,24,512]{2,1,0:T(8,128)S(1)} async-done(((f32[16,24,512]{2,1,0:T(8,128)}), f32[16,24,512]{2,1,0:T(8,128)S(1)}, u32[]{:S(2)}, u32[]{:S(2)}) %all-to-all-start.2) | async-done | bytes 786464 | tf_op jit(solution)/shard_map/all_to_all | solution.py:342
  29.8 0.0 copy-start.1
  29.8 5.4 %all-to-all-start = ((f32[16,24,512]{2,1,0:T(8,128)}), f32[16,24,512]{2,1,0:T(8,128)S(1)}, u32[]{:S(2)}, u32[]{:S(2)}) async-start(f32[16,24,512]{2,1,0:T(8,128)} %shard_map.77), calls=%async_computation | async-start | bytes 1572864 | tf_op jit(solution)/shard_map/all_to_all | solution.py:342
  35.2 0.0 copy-done.1
  35.2 3.5 %shard_map.80 = f32[16,56,128]{2,1,0:T(8,128)} custom-call(f32[16,24,512]{2,1,0:T(8,128)} %copy-done.1, f32[2,16,256]{2,1,0:T(8,128)} %constant.6.clone.twist_ref, bf16[512,512]{1,0:T(8,128)(2,1)} %constant.7.clone.high_ref, bf16[512,512]{1,0:T(8,128)(2,1)} %constant.8.clone.low_ref), custom_call_target="tpu_custom_call" | custom-call | tf_op jit(solution)/shard_map/pallas_call | solution.py:253
  38.6 15.2 %all-to-all-done.x_ref = f32[16,24,512]{2,1,0:T(8,128)S(1)} async-done(((f32[16,24,512]{2,1,0:T(8,128)}), f32[16,24,512]{2,1,0:T(8,128)S(1)}, u32[]{:S(2)}, u32[]{:S(2)}) %all-to-all-start) | async-done | bytes 786464 | tf_op jit(solution)/shard_map/all_to_all | solution.py:342
  53.8 0.0 copy-start
  53.8 5.4 %all-to-all-start.3 = ((f32[16,56,128]{2,1,0:T(8,128)}), f32[16,56,128]{2,1,0:T(8,128)S(1)}, u32[]{:S(2)}, u32[]{:S(2)}) async-start(f32[16,56,128]{2,1,0:T(8,128)} %shard_map.80), calls=%async_computation.3 | async-start | bytes 917504 | tf_op jit(solution)/shard_map/all_to_all | solution.py:346
  59.2 0.0 copy-done
  59.2 3.5 %shard_map.78 = f32[16,56,128]{2,1,0:T(8,128)} custom-call(f32[16,24,512]{2,1,0:T(8,128)} %copy-done, f32[2,16,256]{2,1,0:T(8,128)} %constant.6.clone.twist_ref, bf16[512,512]{1,0:T(8,128)(2,1)} %constant.7.clone.high_ref, bf16[512,512]{1,0:T(8,128)(2,1)} %constant.8.clone.low_ref), custom_call_target="tpu_custom_call" | custom-call | tf_op jit(solution)/shard_map/pallas_call | solution.py:253
  62.7 9.7 %all-to-all-done.3.refs_3_ = f32[16,56,128]{2,1,0:T(8,128)S(1)} async-done(((f32[16,56,128]{2,1,0:T(8,128)}), f32[16,56,128]{2,1,0:T(8,128)S(1)}, u32[]{:S(2)}, u32[]{:S(2)}) %all-to-all-start.3) | async-done | bytes 458784 | tf_op jit(solution)/shard_map/all_to_all | solution.py:346
  72.4 0.0 copy-start.2
  72.4 3.8 %all-to-all-start.1 = ((f32[16,56,128]{2,1,0:T(8,128)}), f32[16,56,128]{2,1,0:T(8,128)S(1)}, u32[]{:S(2)}, u32[]{:S(2)}) async-start(f32[16,56,128]{2,1,0:T(8,128)} %shard_map.78), calls=%async_computation.1 | async-start | bytes 917504 | tf_op jit(solution)/shard_map/all_to_all | solution.py:346
  77.5 11.9 %all-to-all-done.1.refs_2_ = f32[16,56,128]{2,1,0:T(8,128)S(1)} async-done(((f32[16,56,128]{2,1,0:T(8,128)}), f32[16,56,128]{2,1,0:T(8,128)S(1)}, u32[]{:S(2)}, u32[]{:S(2)}) %all-to-all-start.1) | async-done | bytes 458784 | tf_op jit(solution)/shard_map/all_to_all | solution.py:346
  89.5 0.0 copy-done.2
  89.5 0.0 copy-start.3
  89.5 0.8 copy-done.3
  90.2 3.3 %shard_map.81 = (f32[256,768]{1,0:T(8,128)}, f32[256,768]{1,0:T(8,128)}) custom-call(s32[1]{0:T(128)S(6)} %copy.8.refs_0_, s32[1]{0:T(128)S(6)} %copy.9.refs_1_, f32[16,56,128]{2,1,0:T(8,128)} %copy-done.3, f32[16,56,128]{2,1,0:T(8,128)} %copy-done.2), custom_call_target="tpu_custom_call" | custom-call | tf_op jit(solution)/shard_map/pallas_call | solution.py:320
Async XLA Ops:
  3.7 26.1 %all-to-all-start.2 = ((f32[16,24,512]{2,1,0:T(8,128)}), f32[16,24,512]{2,1,0:T(8,128)S(1)}, u32[]{:S(2)}, u32[]{:S(2)}) async-start(f32[16,24,512]{2,1,0:T(8,128)} %shard_map.79), calls=%async_computation.2 | async-start | bytes 1572864 | tf_op jit(solution)/shard_map/all_to_all | solution.py:342
  29.8 5.4 %copy-start.1 = (f32[16,24,512]{2,1,0:T(8,128)}, f32[16,24,512]{2,1,0:T(8,128)S(1)}, u32[]{:S(2)}) copy-start(f32[16,24,512]{2,1,0:T(8,128)S(1)} %all-to-all-done.2.x_ref) | copy-start | bytes 2359300
  29.8 24.1 %all-to-all-start = ((f32[16,24,512]{2,1,0:T(8,128)}), f32[16,24,512]{2,1,0:T(8,128)S(1)}, u32[]{:S(2)}, u32[]{:S(2)}) async-start(f32[16,24,512]{2,1,0:T(8,128)} %shard_map.77), calls=%async_computation | async-start | bytes 1572864 | tf_op jit(solution)/shard_map/all_to_all | solution.py:342
  53.8 5.4 %copy-start = (f32[16,24,512]{2,1,0:T(8,128)}, f32[16,24,512]{2,1,0:T(8,128)S(1)}, u32[]{:S(2)}) copy-start(f32[16,24,512]{2,1,0:T(8,128)S(1)} %all-to-all-done.x_ref) | copy-start | bytes 2359300
  53.8 18.6 %all-to-all-start.3 = ((f32[16,56,128]{2,1,0:T(8,128)}), f32[16,56,128]{2,1,0:T(8,128)S(1)}, u32[]{:S(2)}, u32[]{:S(2)}) async-start(f32[16,56,128]{2,1,0:T(8,128)} %shard_map.80), calls=%async_computation.3 | async-start | bytes 917504 | tf_op jit(solution)/shard_map/all_to_all | solution.py:346
  72.4 17.0 %copy-start.2 = (f32[16,56,128]{2,1,0:T(8,128)}, f32[16,56,128]{2,1,0:T(8,128)S(1)}, u32[]{:S(2)}) copy-start(f32[16,56,128]{2,1,0:T(8,128)S(1)} %all-to-all-done.3.refs_3_) | copy-start | bytes 1376260
  72.4 17.0 %all-to-all-start.1 = ((f32[16,56,128]{2,1,0:T(8,128)}), f32[16,56,128]{2,1,0:T(8,128)S(1)}, u32[]{:S(2)}, u32[]{:S(2)}) async-start(f32[16,56,128]{2,1,0:T(8,128)} %shard_map.78), calls=%async_computation.1 | async-start | bytes 917504 | tf_op jit(solution)/shard_map/all_to_all | solution.py:346
  89.5 0.8 copy-start.3

commit v2 on v1

--- a/solution.py
+++ b/solution.py
@@ -12,7 +12,7 @@
 LANES = 128
 SUBLANES = 8
 EDGE = 8
-CHUNKS = (3, 3)
+CHUNKS = (6,)
 
 
 TWO_PI = 6.283185307179586

time: 94.2 us -> 83.6 us (0.89)
  blocking collectives: 0 us -> 43.4 us
  waiting for transfers between devices: 52.5 us -> 18.4 us
  starting transfers between devices: 22 us -> 5.06 us
  Pallas kernels: 16.3 us -> 12.9 us
    all_to_all x0 -> x1, blocking collectives: none -> 43.4 us  [shards(): lax.all_to_all(spread(echoes, devices, first, count), 'pulse', 0, 0, tile...]
    all_to_all x2 -> x0, waiting for transfers between devices: 30.8 us -> none  [shards(): lax.all_to_all(spread(echoes, devices, first, count), 'pulse', 0, 0, tile...]
    all_to_all x2 -> x0, starting transfers between devices: 12.8 us -> none  [shards(): lax.all_to_all(spread(echoes, devices, first, count), 'pulse', 0, 0, tile...]
    all_to_all x2 -> x1, starting transfers between devices: 9.17 us -> 5.06 us  [shards(): lax.all_to_all(transform(column, tables), 'pulse', 0, 0, tiled=True)]
    all_to_all x2 -> x1, waiting for transfers between devices: 21.7 us -> 18.4 us  [shards(): lax.all_to_all(transform(column, tables), 'pulse', 0, 0, tiled=True)]
    pallas_call x2 -> x1, Pallas kernels: 6.96 us -> 4.79 us  [transform(): pl.pallas_call(transform_kernel, out_shape=jax.ShapeDtypeStruct((devices,...]
    pallas_call x2 -> x1, Pallas kernels: 6.07 us -> 4.88 us  [spread(): pl.pallas_call(spread_kernel, grid=(count,), in_specs=[pl.BlockSpec((part...]
  transfers between devices with their start and end apart: 4 -> 1, of which waited for: 4 -> 1; matrix products, arithmetic and copies ran while one was open for 0% -> 0% of each run, Pallas kernels for 11% -> 0%
where the time goes in v2:
time: 83.6 us; the launch traced here: 82.7 us
  blocking collectives  43.4 us (52%)
  waiting for transfers between devices  18.4 us (22%)
  Pallas kernels  12.9 us (15%)
  starting transfers between devices  5.06 us (6%)
  between operations  1.93 us (2%)
  local copies, waits for them, and re-layouts  0.91 us (1%)
    all_to_all x1, blocking collectives, shards(): lax.all_to_all(spread(echoes, devices, first, count), 'pulse', 0, 0, tile...  43.4 us
    all_to_all x1, waiting for transfers between devices, shards(): lax.all_to_all(transform(column, tables), 'pulse', 0, 0, tiled=True)  18.4 us
    all_to_all x1, starting transfers between devices, shards(): lax.all_to_all(transform(column, tables), 'pulse', 0, 0, tiled=True)  5.06 us
    pallas_call x1, Pallas kernels, spread(): pl.pallas_call(spread_kernel, grid=(count,), in_specs=[pl.BlockSpec((part...  4.88 us
    pallas_call x1, Pallas kernels, transform(): pl.pallas_call(transform_kernel, out_shape=jax.ShapeDtypeStruct((devices,...  4.79 us
    pallas_call x1, Pallas kernels, finish(): pl.pallas_call(body, in_specs=[smem, smem] + [vmem] * len(blocks), out_sp...  3.28 us
  transfers between devices with their start and end apart: 1, of which 1 were waited for; matrix products, arithmetic and copies ran while one was open for 0% of the time, Pallas kernels for 0%

profile of v2, /device:TPU:0, one launch (start us, length us, event | category | flops | bytes accessed | tf_op | source)
XLA Modules:
  0.0 82.7 jit_solution(13794859925094119972)
XLA Ops:
  0.6 4.9 %shard_map.77 = f32[16,48,512]{2,1,0:T(8,128)} custom-call(f32[2,256,768]{2,1,0:T(8,128)} %x_ref.1), custom_call_target="tpu_custom_call" | custom-call | tf_op jit(solution)/shard_map/pallas_call | solution.py:138
  5.5 43.4 %all_to_all.10.x_ref = f32[16,48,512]{2,1,0:T(8,128)} all-to-all(f32[16,48,512]{2,1,0:T(8,128)} %shard_map.77), channel_id=1, replica_groups=mesh['beam'=2,'pulse'=16] {'pulse'}, dimensions={0} | all-to-all | bytes 3145728 | tf_op jit(solution)/shard_map/all_to_all | solution.py:342
  48.9 4.8 %shard_map.78 = f32[16,104,128]{2,1,0:T(8,128)} custom-call(f32[16,48,512]{2,1,0:T(8,128)} %all_to_all.10.x_ref, f32[2,16,256]{2,1,0:T(8,128)} %constant.6.clone.twist_ref, bf16[512,512]{1,0:T(8,128)(2,1)} %constant.7.clone.high_ref, bf16[512,512]{1,0:T(8,128)(2,1)} %constant.8.clone.low_ref), custom_call_target="tpu_custom_call" | custom-call | tf_op jit(solution)/shard_map/pallas_call | solution.py:253
  53.7 5.1 %all-to-all-start.1 = ((f32[16,104,128]{2,1,0:T(8,128)}), f32[16,104,128]{2,1,0:T(8,128)S(1)}, u32[]{:S(2)}, u32[]{:S(2)}) async-start(f32[16,104,128]{2,1,0:T(8,128)} %shard_map.78), calls=%async_computation.1 | async-start | bytes 1703936 | tf_op jit(solution)/shard_map/all_to_all | solution.py:346
  60.1 18.4 %all-to-all-done.1.refs_2_ = f32[16,104,128]{2,1,0:T(8,128)S(1)} async-done(((f32[16,104,128]{2,1,0:T(8,128)}), f32[16,104,128]{2,1,0:T(8,128)S(1)}, u32[]{:S(2)}, u32[]{:S(2)}) %all-to-all-start.1) | async-done | bytes 852000 | tf_op jit(solution)/shard_map/all_to_all | solution.py:346
  78.5 0.0 copy-start
  78.5 0.9 %copy-done = f32[16,104,128]{2,1,0:T(8,128)} copy-done((f32[16,104,128]{2,1,0:T(8,128)}, f32[16,104,128]{2,1,0:T(8,128)S(1)}, u32[]{:S(2)}) %copy-start) | copy-done | bytes 851992
  79.4 3.3 %shard_map.79 = (f32[256,768]{1,0:T(8,128)}, f32[256,768]{1,0:T(8,128)}) custom-call(s32[1]{0:T(128)S(6)} %copy.8.refs_0_, s32[1]{0:T(128)S(6)} %copy.9.refs_1_, f32[16,104,128]{2,1,0:T(8,128)} %copy-done), custom_call_target="tpu_custom_call" | custom-call | tf_op jit(solution)/shard_map/pallas_call | solution.py:320
Async XLA Ops:
  53.7 24.8 %all-to-all-start.1 = ((f32[16,104,128]{2,1,0:T(8,128)}), f32[16,104,128]{2,1,0:T(8,128)S(1)}, u32[]{:S(2)}, u32[]{:S(2)}) async-start(f32[16,104,128]{2,1,0:T(8,128)} %shard_map.78), calls=%async_computation.1 | async-start | bytes 1703936 | tf_op jit(solution)/shard_map/all_to_all | solution.py:346
  78.5 0.9 %copy-start = (f32[16,104,128]{2,1,0:T(8,128)}, f32[16,104,128]{2,1,0:T(8,128)S(1)}, u32[]{:S(2)}) copy-start(f32[16,104,128]{2,1,0:T(8,128)S(1)} %all-to-all-done.1.refs_2_) | copy-start | bytes 2555908
